TPU v7x, 32 devices: a whole 2x2x4 slice. The times are simulated.
32 devices in a mesh: level: 4 (over y, core), blk: 8 (over z, x).
Axes of the slice: x: 2, y: 2, z: 4, core: 2. Of those that a mesh axis runs over, the one named last changes fastest.
Arguments:
- right_sides: bfloat16 [4, 8, 1024, 384], P('level', 'blk'), may hold values from -6 to 6
- diag_inverse: bfloat16 [4, 8, 1, 1024, 1024], P('level', 'blk'), may hold values from -0.1875 to 0.1875
- compress_basis: bfloat16 [4, 8, 1024, 256], P('level', 'blk'), may hold values from -0.1875 to 0.1875
- expand_basis: bfloat16 [4, 8, 1024, 256], P('level', 'blk'), may hold values from -0.125 to 0.125
- target_ranks: int32 [4, 8], P('level', 'blk'), may hold values from 32 to 256
- coupling: int32 [4, 8, 4, 8], replicated, may hold values 0 or 1
- section_order: int32 [4], replicated, may hold values from 0 to 3, each once
Outputs:
- solved: bfloat16 [4, 8, 1024, 384], P('level', 'blk')
All inputs are finite; a program needn't handle non-finite values.
Results may differ from a plain program's by a relative error of at most 0.015.
Values may be sent and summed in bfloat16 or wider, within the bound.
No kernel may reach another device: no remote copies, remote signals or barrier semaphores. Data moves between devices by JAX's collectives and lax.ppermute only.
A program may use at most 128 MiB of HBM per device.

v0:
```python
import jax
import jax.numpy as jnp
from jax import lax
from jax.sharding import PartitionSpec as P


def per_device(
    right_sides, diag_inverse, compress_basis, expand_basis, target_ranks, coupling, section_order
):
    levels = lax.axis_size("level")
    blocks = lax.axis_size("blk")
    my_level = lax.axis_index("level")
    my_block = lax.axis_index("blk")
    sides_here = right_sides[0, 0]
    inverse_here = diag_inverse[0, 0]
    basis_here = compress_basis[0, 0]
    expand_here = expand_basis[0, 0]
    rank_cap = basis_here.shape[1]
    seg_rows = sides_here.shape[0]
    sub_blocks = inverse_here.shape[0]
    block_rows = inverse_here.shape[1]
    kept_rows = (jnp.arange(rank_cap, dtype=jnp.int32) < target_ranks[0, 0])[:, None]
    my_section = section_order[my_level]
    level_ids = jnp.arange(levels, dtype=jnp.int32)

    def solve(incoming, columns):
        update = jnp.dot(
            expand_here, incoming.astype(jnp.bfloat16), preferred_element_type=jnp.float32
        )
        work_rows = (columns.astype(jnp.float32) - update).astype(jnp.bfloat16)
        work_rows = work_rows.reshape(sub_blocks, block_rows, columns.shape[1])
        solved_rows = jnp.einsum(
            "jab,jbr->jar", inverse_here, work_rows, preferred_element_type=jnp.float32
        )
        solved_rows = solved_rows.astype(jnp.bfloat16).reshape(seg_rows, columns.shape[1])
        coef_rows = lax.dot_general(
            basis_here, solved_rows, (((0,), (0,)), ((), ())), preferred_element_type=jnp.float32
        )
        coef_rows = jnp.where(kept_rows, coef_rows, 0.0).astype(jnp.bfloat16)
        return (solved_rows, coef_rows)

    def advance(carry_state, level_step, columns):
        incoming, solved_rows, coef_rows = carry_state
        solved_rows, coef_rows = lax.cond(
            my_section == level_step,
            lambda: solve(incoming, columns),
            lambda: (solved_rows, coef_rows),
        )
        if level_step == levels - 1:
            return (incoming, solved_rows, coef_rows)
        root_level = jnp.sum(jnp.where(section_order == level_step, level_ids, 0))
        is_later = (my_section > level_step).astype(jnp.float32)
        width_now = columns.shape[1]
        masked = jnp.where(my_level == root_level, coef_rows.astype(jnp.float32), 0.0)
        share = lax.psum_scatter(
            masked.astype(jnp.bfloat16), "level", scatter_dimension=1, tiled=True
        )
        share_cols = share.shape[1]
        gathered = lax.all_gather(share[None], "blk", axis=0, tiled=True)
        dest_weights = coupling[:, my_block, root_level, :].astype(jnp.bfloat16)
        sums = jnp.dot(
            dest_weights, gathered.reshape(blocks, -1), preferred_element_type=jnp.float32
        )
        sums = sums.reshape(levels, rank_cap, share_cols)
        arrived = lax.all_to_all(sums, "level", split_axis=0, concat_axis=2, tiled=True)
        arrived = arrived.reshape(rank_cap, width_now)
        return (incoming + is_later * arrived, solved_rows, coef_rows)

    width_now = sides_here.shape[1]
    carry_state = (
        jnp.zeros((rank_cap, width_now), jnp.float32),
        jnp.zeros((seg_rows, width_now), jnp.bfloat16),
        jnp.zeros((rank_cap, width_now), jnp.bfloat16),
    )
    for level_step in range(levels):
        carry_state = advance(carry_state, level_step, sides_here)
    result = carry_state[1]
    return result[None, None]


def solution(mesh):
    return jax.shard_map(
        per_device,
        mesh=mesh,
        in_specs=(
            P("level", "blk", None, None),
            P("level", "blk", None, None, None),
            P("level", "blk", None, None),
            P("level", "blk", None, None),
            P("level", "blk"),
            P(),
            P(),
        ),
        out_specs=P("level", "blk", None, None),
        check_vma=False,
    )
```

profile of v0, /device:TPU:1, one launch (start us, length us, event | category | flops | bytes accessed | tf_op | source)
XLA Modules:
  0.0 240.1 jit_solution(6065074242285254970)
XLA Ops:
  6.5 1.5 fusion.52
  8.0 1.3 dynamic_slice.12
  10.0 1.4 copy.24
  12.8 1.0 conditional.4
  12.8 1.0 broadcast_in_dim.52
  20.5 0.8 dynamic-slice_convert_fusion
  21.4 18.5 %reduce-scatter.4.cloned.1.call-done = bf16[256,96]{0,1:T(8,128)(2,1)} async-done(((bf16[256,384]{0,1:T(8,128)(2,1)}), bf16[256,96]{0,1:T(8,128)(2,1)}) %reduce-scatter.4.cloned.1.call-update) | async-done | bytes 49168 | tf_op jit(solution)/shard_map/reduce_scatter | solution.py:55
  39.9 25.3 %all-gather = bf16[2048,96]{0,1:T(8,128)(2,1)S(1)} all-gather(bf16[256,96]{0,1:T(8,128)(2,1)} %reduce-scatter.4.cloned.1.call-done), channel_id=2, replica_groups=mesh['level'=4,'blk'=8] {'blk'}, dimensions={0}, use_global_device_ids=true | all-gather | bytes 442368 | tf_op jit(solution)/shard_map/all_gather | solution.py:59
  67.4 0.8 copy.27
  68.2 10.6 %all-to-all-start = ((f32[4,256,96]{1,2,0:T(8,128)}), f32[4,256,96]{1,2,0:T(8,128)S(1)}, u32[]{:S(2)}, u32[]{:S(2)}) async-start(f32[4,256,96]{1,2,0:T(8,128)} %copy.27), calls=%async_computation.1 | async-start | bytes 786432 | tf_op jit(solution)/shard_map/all_to_all | solution.py:65
  80.7 4.5 %all-to-all-done = f32[4,256,96]{1,2,0:T(8,128)S(1)} async-done(((f32[4,256,96]{1,2,0:T(8,128)}), f32[4,256,96]{1,2,0:T(8,128)S(1)}, u32[]{:S(2)}, u32[]{:S(2)}) %all-to-all-start) | async-done | bytes 393248 | tf_op jit(solution)/shard_map/all_to_all | solution.py:65
  86.0 25.5 %reduce-scatter.6.cloned.1.call-done = bf16[256,96]{0,1:T(8,128)(2,1)} async-done(((bf16[256,384]{0,1:T(8,128)(2,1)}), bf16[256,96]{0,1:T(8,128)(2,1)}) %reduce-scatter.6.cloned.1.call-update) | async-done | bytes 49168 | tf_op jit(solution)/shard_map/reduce_scatter | solution.py:55
  111.5 25.3 %all-gather.1 = bf16[2048,96]{0,1:T(8,128)(2,1)S(1)} all-gather(bf16[256,96]{0,1:T(8,128)(2,1)} %reduce-scatter.6.cloned.1.call-done), channel_id=3, replica_groups=mesh['level'=4,'blk'=8] {'blk'}, dimensions={0}, use_global_device_ids=true | all-gather | bytes 442368 | tf_op jit(solution)/shard_map/all_gather | solution.py:59
  138.9 0.8 copy.32
  139.8 10.7 %all-to-all-start.1 = ((f32[4,256,96]{1,2,0:T(8,128)}), f32[4,256,96]{1,2,0:T(8,128)S(1)}, u32[]{:S(2)}, u32[]{:S(2)}) async-start(f32[4,256,96]{1,2,0:T(8,128)} %copy.32), calls=%async_computation.3 | async-start | bytes 786432 | tf_op jit(solution)/shard_map/all_to_all | solution.py:65
  152.5 4.4 %all-to-all-done.1 = f32[4,256,96]{1,2,0:T(8,128)S(1)} async-done(((f32[4,256,96]{1,2,0:T(8,128)}), f32[4,256,96]{1,2,0:T(8,128)S(1)}, u32[]{:S(2)}, u32[]{:S(2)}) %all-to-all-start.1) | async-done | bytes 393248 | tf_op jit(solution)/shard_map/all_to_all | solution.py:65
  157.7 25.5 %reduce-scatter.8.cloned.1.call-done = bf16[256,96]{0,1:T(8,128)(2,1)} async-done(((bf16[256,384]{0,1:T(8,128)(2,1)}), bf16[256,96]{0,1:T(8,128)(2,1)}) %reduce-scatter.8.cloned.1.call-update) | async-done | bytes 49168 | tf_op jit(solution)/shard_map/reduce_scatter | solution.py:55
  183.3 25.5 %all-gather.2 = bf16[2048,96]{0,1:T(8,128)(2,1)S(1)} all-gather(bf16[256,96]{0,1:T(8,128)(2,1)} %reduce-scatter.8.cloned.1.call-done), channel_id=4, replica_groups=mesh['level'=4,'blk'=8] {'blk'}, dimensions={0}, use_global_device_ids=true | all-gather | bytes 442368 | tf_op jit(solution)/shard_map/all_gather | solution.py:59
  211.0 0.8 copy.37
  211.8 10.5 %all-to-all-start.2 = ((f32[4,256,96]{1,2,0:T(8,128)}), f32[4,256,96]{1,2,0:T(8,128)S(1)}, u32[]{:S(2)}, u32[]{:S(2)}) async-start(f32[4,256,96]{1,2,0:T(8,128)} %copy.37), calls=%async_computation.5 | async-start | bytes 786432 | tf_op jit(solution)/shard_map/all_to_all | solution.py:65
  223.0 5.8 %all-to-all-done.2 = f32[4,256,96]{1,2,0:T(8,128)S(1)} async-done(((f32[4,256,96]{1,2,0:T(8,128)}), f32[4,256,96]{1,2,0:T(8,128)S(1)}, u32[]{:S(2)}, u32[]{:S(2)}) %all-to-all-start.2) | async-done | bytes 393248 | tf_op jit(solution)/shard_map/all_to_all | solution.py:65
  228.8 3.9 %conditional.7 = (bf16[1,1,1024,384]{3,2,1,0:T(8,128)(2,1)S(1)}) conditional(s32[]{:T(128)} %bitcast.17, bf16[1024,384]{0,1:T(8,128)(2,1)} %get-tuple-element.110, (bf16[1024,384]{0,1:T(8,128)(2,1)S(1)}, s32[1]{0:T(128)}, f32[1,256,4,96]{1,3,2,0:T(8,128)S(1)}, f32[256,384]{0,1:T(8,128)S(1)}, bf16[1024,256]{1,0:T(8,128)(2,1)S(1)}, ...), branch_computations={%region_12.13_spmd, %region_13.14_spmd} | conditional | flops 1008500736 | bytes 7733274 | solution.py:44
  229.5 2.8 %fusion.6 = bf16[1,1,1024,384]{2,3,1,0:T(8,128)(2,1)S(1)} fusion(bf16[1,1024,1024]{2,1,0:T(8,128)(2,1)} %get-tuple-element.103, bf16[1024,384]{0,1:T(8,128)(2,1)S(1)} %get-tuple-element.98, bf16[256,384]{0,1:T(8,128)(2,1)S(1)} %fusion.9, bf16[1024,256]{1,0:T(8,128)(2,1)S(1)} %get-tuple-element.102), kind=kOutput, calls=%fused_computation.5 | convolution fusion | flops 1008205824 | bytes 4390912 | tf_op jit(solution)/shard_map/cond/branch_1_fun/jab,jbr->jar/dot_general | solution.py:32
  232.7 0.9 copy-done
  (43 shorter events, 9.2 us)
Async XLA Ops:
  6.5 6.2 %copy-start.2 = (bf16[1,1,1024,256]{3,2,1,0:T(8,128)(2,1)S(1)}, bf16[1,1,1024,256]{3,2,1,0:T(8,128)(2,1)}, u32[]{:S(2)}) copy-start(bf16[1,1,1024,256]{3,2,1,0:T(8,128)(2,1)} %param.18) | copy-start | bytes 1572868
  6.5 6.2 %copy-start.1 = (bf16[1,1,1024,256]{3,2,1,0:T(8,128)(2,1)S(1)}, bf16[1,1,1024,256]{3,2,1,0:T(8,128)(2,1)}, u32[]{:S(2)}) copy-start(bf16[1,1,1024,256]{3,2,1,0:T(8,128)(2,1)} %param.17) | copy-start | bytes 1572868
  6.5 33.3 %reduce-scatter.4.cloned.1.call-start = ((), (), s32[]{:S(2)}) async-start(), calls=%async_computation.6 | async-start | bytes 245760 | tf_op jit(solution)/shard_map/reduce_scatter | solution.py:55
  68.2 17.0 %all-to-all-start = ((f32[4,256,96]{1,2,0:T(8,128)}), f32[4,256,96]{1,2,0:T(8,128)S(1)}, u32[]{:S(2)}, u32[]{:S(2)}) async-start(f32[4,256,96]{1,2,0:T(8,128)} %copy.27), calls=%async_computation.1 | async-start | bytes 786432 | tf_op jit(solution)/shard_map/all_to_all | solution.py:65
  78.8 32.7 %reduce-scatter.6.cloned.1.call-start = ((), (), s32[]{:S(2)}) async-start(), calls=%async_computation.7 | async-start | bytes 245760 | tf_op jit(solution)/shard_map/reduce_scatter | solution.py:55
  139.8 17.2 %copy-start.3 = (bf16[1,1,1024,256]{3,2,1,0:T(8,128)(2,1)S(1)}, bf16[1,1,1024,256]{3,2,1,0:T(8,128)(2,1)}, u32[]{:S(2)}) copy-start(bf16[1,1,1024,256]{3,2,1,0:T(8,128)(2,1)} %param.18) | copy-start | bytes 1572868
  139.8 17.1 %all-to-all-start.1 = ((f32[4,256,96]{1,2,0:T(8,128)}), f32[4,256,96]{1,2,0:T(8,128)S(1)}, u32[]{:S(2)}, u32[]{:S(2)}) async-start(f32[4,256,96]{1,2,0:T(8,128)} %copy.32), calls=%async_computation.3 | async-start | bytes 786432 | tf_op jit(solution)/shard_map/all_to_all | solution.py:65
  150.5 32.8 %reduce-scatter.8.cloned.1.call-start = ((), (), s32[]{:S(2)}) async-start(), calls=%async_computation.8 | async-start | bytes 245760 | tf_op jit(solution)/shard_map/reduce_scatter | solution.py:55
  210.4 18.4 %copy-start.4 = (bf16[1,1,1024,256]{3,2,1,0:T(8,128)(2,1)S(1)}, bf16[1,1,1024,256]{3,2,1,0:T(8,128)(2,1)}, u32[]{:S(2)}) copy-start(bf16[1,1,1024,256]{3,2,1,0:T(8,128)(2,1)} %param.18) | copy-start | bytes 1572868
  211.8 17.0 %all-to-all-start.2 = ((f32[4,256,96]{1,2,0:T(8,128)}), f32[4,256,96]{1,2,0:T(8,128)S(1)}, u32[]{:S(2)}, u32[]{:S(2)}) async-start(f32[4,256,96]{1,2,0:T(8,128)} %copy.37), calls=%async_computation.5 | async-start | bytes 786432 | tf_op jit(solution)/shard_map/all_to_all | solution.py:65
  232.7 0.9 copy-start
Sparse Core Ops, SparseCore 0:
  14.6 25.2 reduce-scatter.3
  86.1 25.3 reduce-scatter.5
  157.9 25.3 reduce-scatter.7
where the time goes:
time: 241 us; the launch traced here: 240 us
  waiting for transfers between devices  84.2 us (35%)
  blocking collectives  76.2 us (32%)
  starting transfers between devices  31.8 us (13%)
  between operations  26 us (11%)
  local copies, waits for them, and re-layouts  13 us (5%)
  other arithmetic  4.62 us (2%)
  matrix products  3.55 us (1%)
    all_gather x3, blocking collectives, advance(): gathered = lax.all_gather(share[None], 'blk', axis=0, tiled=True)  76.2 us
    reduce_scatter x3, waiting for transfers between devices, advance(): lax.psum_scatter(masked.astype(jnp.bfloat16), 'level', scatter_dimension=...  69.5 us
    all_to_all x3, starting transfers between devices, advance(): lax.all_to_all(sums, 'level', split_axis=0, concat_axis=2, tiled=True)  31.8 us
    all_to_all x3, waiting for transfers between devices, advance(): lax.all_to_all(sums, 'level', split_axis=0, concat_axis=2, tiled=True)  14.6 us
    dot_general x9, local copies, waits for them, and re-layouts, advance(): jnp.dot(dest_weights, gathered.reshape(blocks, -1), preferred_element_typ...  5.09 us
  transfers between devices with their start and end apart: 6, of which 6 were waited for; matrix products, arithmetic and copies ran while one was open for 0% of the time, Pallas kernels for 0%

commit v1 on v0

--- a/solution.py
+++ b/solution.py
@@ -62,7 +62,15 @@
             dest_weights, gathered.reshape(blocks, -1), preferred_element_type=jnp.float32
         )
         sums = sums.reshape(levels, rank_cap, share_cols)
-        arrived = lax.all_to_all(sums, "level", split_axis=0, concat_axis=2, tiled=True)
+        arrived = jnp.concatenate(
+            lax.all_to_all(
+                jnp.stack(jnp.split(sums, lax.axis_size("level"), axis=0), axis=0),
+                axis_name="level",
+                split_axis=0,
+                concat_axis=0,
+            ),
+            axis=2,
+        )
         arrived = arrived.reshape(rank_cap, width_now)
         return (incoming + is_later * arrived, solved_rows, coef_rows)
 

time: 241 us -> 243 us (level)
    dot_general x9 -> x0, local copies, waits for them, and re-layouts: 5.09 us -> none  [advance(): jnp.dot(dest_weights, gathered.reshape(blocks, -1), preferred_element_typ...]
    another operation x0 -> x15, local copies, waits for them, and re-layouts: none -> 3.88 us  [advance(): jnp.stack(jnp.split(sums, lax.axis_size('level'), axis=0), axis=0)]
    split x0 -> x3, local copies, waits for them, and re-layouts: none -> 3.27 us  [advance(): jnp.split(sums, lax.axis_size('level'), axis=0)]
where the time goes in v1:
time: 243 us; the launch traced here: 242 us
  waiting for transfers between devices  84.6 us (35%)
  blocking collectives  75.9 us (31%)
  starting transfers between devices  31.9 us (13%)
  between operations  25.5 us (10%)
  local copies, waits for them, and re-layouts  15.1 us (6%)
  other arithmetic  4.76 us (2%)
  matrix products  3.56 us (1%)
    all_gather x3, blocking collectives, advance(): gathered = lax.all_gather(share[None], 'blk', axis=0, tiled=True)  75.9 us
    reduce_scatter x3, waiting for transfers between devices, advance(): lax.psum_scatter(masked.astype(jnp.bfloat16), 'level', scatter_dimension=...  69.7 us
    all_to_all x3, starting transfers between devices, advance(): lax.all_to_all(jnp.stack(jnp.split(sums, lax.axis_size('level'), axis=0),...  31.9 us
    all_to_all x3, waiting for transfers between devices, advance(): lax.all_to_all(jnp.stack(jnp.split(sums, lax.axis_size('level'), axis=0),...  14.9 us
  transfers between devices with their start and end apart: 6, of which 6 were waited for; matrix products, arithmetic and copies ran while one was open for 0% of the time, Pallas kernels for 0%

profile of v1, /device:TPU:1, one launch (start us, length us, event | category | flops | bytes accessed | tf_op | source)
XLA Modules:
  0.0 242.3 jit_solution(7633553309865791386)
XLA Ops:
  6.5 1.5 fusion.52
  8.0 1.3 dynamic_slice.12
  10.0 1.4 copy.26
  12.7 1.0 conditional.4
  12.7 1.0 broadcast_in_dim.52
  21.1 18.7 %reduce-scatter.4.cloned.1.call-done = bf16[256,96]{0,1:T(8,128)(2,1)} async-done(((bf16[256,384]{0,1:T(8,128)(2,1)}), bf16[256,96]{0,1:T(8,128)(2,1)}) %reduce-scatter.4.cloned.1.call-update) | async-done | bytes 49168 | tf_op jit(solution)/shard_map/reduce_scatter | solution.py:55
  39.8 25.3 %all-gather = bf16[2048,96]{0,1:T(8,128)(2,1)S(1)} all-gather(bf16[256,96]{0,1:T(8,128)(2,1)} %reduce-scatter.4.cloned.1.call-done), channel_id=2, replica_groups=mesh['level'=4,'blk'=8] {'blk'}, dimensions={0}, use_global_device_ids=true | all-gather | bytes 442368 | tf_op jit(solution)/shard_map/all_gather | solution.py:59
  66.4 1.1 slice_reduce_fusion.11
  68.0 0.9 copy.28
  68.9 10.6 %all-to-all-start = ((f32[4,1,256,96]{2,3,1,0:T(8,128)}), f32[4,1,256,96]{2,3,1,0:T(8,128)S(1)}, u32[]{:S(2)}, u32[]{:S(2)}) async-start(f32[4,1,256,96]{2,3,1,0:T(8,128)} %copy.28), calls=%async_computation.1 | async-start | bytes 786432 | tf_op jit(solution)/shard_map/all_to_all | solution.py:66
  81.4 4.5 %all-to-all-done = f32[4,1,256,96]{2,3,1,0:T(8,128)S(1)} async-done(((f32[4,1,256,96]{2,3,1,0:T(8,128)}), f32[4,1,256,96]{2,3,1,0:T(8,128)S(1)}, u32[]{:S(2)}, u32[]{:S(2)}) %all-to-all-start) | async-done | bytes 393248 | tf_op jit(solution)/shard_map/all_to_all | solution.py:66
  86.7 25.5 %reduce-scatter.6.cloned.1.call-done = bf16[256,96]{0,1:T(8,128)(2,1)} async-done(((bf16[256,384]{0,1:T(8,128)(2,1)}), bf16[256,96]{0,1:T(8,128)(2,1)}) %reduce-scatter.6.cloned.1.call-update) | async-done | bytes 49168 | tf_op jit(solution)/shard_map/reduce_scatter | solution.py:55
  112.2 25.3 %all-gather.1 = bf16[2048,96]{0,1:T(8,128)(2,1)S(1)} all-gather(bf16[256,96]{0,1:T(8,128)(2,1)} %reduce-scatter.6.cloned.1.call-done), channel_id=3, replica_groups=mesh['level'=4,'blk'=8] {'blk'}, dimensions={0}, use_global_device_ids=true | all-gather | bytes 442368 | tf_op jit(solution)/shard_map/all_gather | solution.py:59
  138.8 1.1 slice_reduce_fusion.7
  140.3 0.9 copy.33
  141.2 10.7 %all-to-all-start.1 = ((f32[4,1,256,96]{2,3,1,0:T(8,128)}), f32[4,1,256,96]{2,3,1,0:T(8,128)S(1)}, u32[]{:S(2)}, u32[]{:S(2)}) async-start(f32[4,1,256,96]{2,3,1,0:T(8,128)} %copy.33), calls=%async_computation.3 | async-start | bytes 786432 | tf_op jit(solution)/shard_map/all_to_all | solution.py:66
  153.8 4.6 %all-to-all-done.1 = f32[4,1,256,96]{2,3,1,0:T(8,128)S(1)} async-done(((f32[4,1,256,96]{2,3,1,0:T(8,128)}), f32[4,1,256,96]{2,3,1,0:T(8,128)S(1)}, u32[]{:S(2)}, u32[]{:S(2)}) %all-to-all-start.1) | async-done | bytes 393248 | tf_op jit(solution)/shard_map/all_to_all | solution.py:66
  159.4 25.5 %reduce-scatter.8.cloned.1.call-done = bf16[256,96]{0,1:T(8,128)(2,1)} async-done(((bf16[256,384]{0,1:T(8,128)(2,1)}), bf16[256,96]{0,1:T(8,128)(2,1)}) %reduce-scatter.8.cloned.1.call-update) | async-done | bytes 49168 | tf_op jit(solution)/shard_map/reduce_scatter | solution.py:55
  184.9 25.3 %all-gather.2 = bf16[2048,96]{0,1:T(8,128)(2,1)S(1)} all-gather(bf16[256,96]{0,1:T(8,128)(2,1)} %reduce-scatter.8.cloned.1.call-done), channel_id=4, replica_groups=mesh['level'=4,'blk'=8] {'blk'}, dimensions={0}, use_global_device_ids=true | all-gather | bytes 442368 | tf_op jit(solution)/shard_map/all_gather | solution.py:59
  211.4 1.1 slice_reduce_fusion.3
  213.9 10.6 %all-to-all-start.2 = ((f32[4,1,256,96]{2,3,1,0:T(8,128)}), f32[4,1,256,96]{2,3,1,0:T(8,128)S(1)}, u32[]{:S(2)}, u32[]{:S(2)}) async-start(f32[4,1,256,96]{2,3,1,0:T(8,128)} %copy.38), calls=%async_computation.5 | async-start | bytes 786432 | tf_op jit(solution)/shard_map/all_to_all | solution.py:66
  225.1 5.8 %all-to-all-done.2 = f32[4,1,256,96]{2,3,1,0:T(8,128)S(1)} async-done(((f32[4,1,256,96]{2,3,1,0:T(8,128)}), f32[4,1,256,96]{2,3,1,0:T(8,128)S(1)}, u32[]{:S(2)}, u32[]{:S(2)}) %all-to-all-start.2) | async-done | bytes 393248 | tf_op jit(solution)/shard_map/all_to_all | solution.py:66
  230.9 3.9 %conditional.7 = (bf16[1,1,1024,384]{3,2,1,0:T(8,128)(2,1)S(1)}) conditional(s32[]{:T(128)} %bitcast.18, bf16[1024,384]{0,1:T(8,128)(2,1)} %get-tuple-element.110, (bf16[1024,384]{0,1:T(8,128)(2,1)S(1)}, s32[1]{0:T(128)}, f32[1,256,4,96]{1,3,0,2:T(8,128)S(1)}, f32[256,384]{0,1:T(8,128)S(1)}, bf16[1024,256]{1,0:T(8,128)(2,1)S(1)}, ...), branch_computations={%region_12.13_spmd, %region_13.14_spmd} | conditional | flops 1008500736 | bytes 7733274 | solution.py:44
  231.7 2.8 %fusion.6 = bf16[1,1,1024,384]{2,3,1,0:T(8,128)(2,1)S(1)} fusion(bf16[1,1024,1024]{2,1,0:T(8,128)(2,1)} %get-tuple-element.103, bf16[1024,384]{0,1:T(8,128)(2,1)S(1)} %get-tuple-element.98, bf16[256,384]{0,1:T(8,128)(2,1)S(1)} %fusion.9, bf16[1024,256]{1,0:T(8,128)(2,1)S(1)} %get-tuple-element.102), kind=kOutput, calls=%fused_computation.5 | convolution fusion | flops 1008205824 | bytes 4390912 | tf_op jit(solution)/shard_map/cond/branch_1_fun/jab,jbr->jar/dot_general | solution.py:32
  (55 shorter events, 10.6 us)
Async XLA Ops:
  6.5 6.1 %copy-start.2 = (bf16[1,1,1024,256]{3,2,1,0:T(8,128)(2,1)S(1)}, bf16[1,1,1024,256]{3,2,1,0:T(8,128)(2,1)}, u32[]{:S(2)}) copy-start(bf16[1,1,1024,256]{3,2,1,0:T(8,128)(2,1)} %param.18) | copy-start | bytes 1572868
  6.5 6.2 %copy-start.1 = (bf16[1,1,1024,256]{3,2,1,0:T(8,128)(2,1)S(1)}, bf16[1,1,1024,256]{3,2,1,0:T(8,128)(2,1)}, u32[]{:S(2)}) copy-start(bf16[1,1,1024,256]{3,2,1,0:T(8,128)(2,1)} %param.17) | copy-start | bytes 1572868
  6.5 33.3 %reduce-scatter.4.cloned.1.call-start = ((), (), s32[]{:S(2)}) async-start(), calls=%async_computation.6 | async-start | bytes 245760 | tf_op jit(solution)/shard_map/reduce_scatter | solution.py:55
  68.9 17.0 %all-to-all-start = ((f32[4,1,256,96]{2,3,1,0:T(8,128)}), f32[4,1,256,96]{2,3,1,0:T(8,128)S(1)}, u32[]{:S(2)}, u32[]{:S(2)}) async-start(f32[4,1,256,96]{2,3,1,0:T(8,128)} %copy.28), calls=%async_computation.1 | async-start | bytes 786432 | tf_op jit(solution)/shard_map/all_to_all | solution.py:66
  79.5 32.7 %reduce-scatter.6.cloned.1.call-start = ((), (), s32[]{:S(2)}) async-start(), calls=%async_computation.7 | async-start | bytes 245760 | tf_op jit(solution)/shard_map/reduce_scatter | solution.py:55
  141.2 17.2 %copy-start.3 = (bf16[1,1,1024,256]{3,2,1,0:T(8,128)(2,1)S(1)}, bf16[1,1,1024,256]{3,2,1,0:T(8,128)(2,1)}, u32[]{:S(2)}) copy-start(bf16[1,1,1024,256]{3,2,1,0:T(8,128)(2,1)} %param.18) | copy-start | bytes 1572868
  141.2 17.1 %all-to-all-start.1 = ((f32[4,1,256,96]{2,3,1,0:T(8,128)}), f32[4,1,256,96]{2,3,1,0:T(8,128)S(1)}, u32[]{:S(2)}, u32[]{:S(2)}) async-start(f32[4,1,256,96]{2,3,1,0:T(8,128)} %copy.33), calls=%async_computation.3 | async-start | bytes 786432 | tf_op jit(solution)/shard_map/all_to_all | solution.py:66
  151.9 33.0 %reduce-scatter.8.cloned.1.call-start = ((), (), s32[]{:S(2)}) async-start(), calls=%async_computation.8 | async-start | bytes 245760 | tf_op jit(solution)/shard_map/reduce_scatter | solution.py:55
  212.7 18.3 %copy-start.4 = (bf16[1,1,1024,256]{3,2,1,0:T(8,128)(2,1)S(1)}, bf16[1,1,1024,256]{3,2,1,0:T(8,128)(2,1)}, u32[]{:S(2)}) copy-start(bf16[1,1,1024,256]{3,2,1,0:T(8,128)(2,1)} %param.18) | copy-start | bytes 1572868
  213.9 17.1 %all-to-all-start.2 = ((f32[4,1,256,96]{2,3,1,0:T(8,128)}), f32[4,1,256,96]{2,3,1,0:T(8,128)S(1)}, u32[]{:S(2)}, u32[]{:S(2)}) async-start(f32[4,1,256,96]{2,3,1,0:T(8,128)} %copy.38), calls=%async_computation.5 | async-start | bytes 786432 | tf_op jit(solution)/shard_map/all_to_all | solution.py:66
  234.8 0.9 copy-start
Sparse Core Ops, SparseCore 0:
  14.6 25.2 reduce-scatter.3
  86.8 25.3 reduce-scatter.5
  159.5 25.3 reduce-scatter.7
